TPU v7x, 32 devices: a whole 2x2x4 slice. The times are simulated.
32 devices in a mesh: head: 8 (over z, y), ctx: 4 (over x, core).
Axes of the slice: x: 2, y: 2, z: 4, core: 2. Of those that a mesh axis runs over, the one named last changes fastest.
Arguments:
- query: bfloat16 [3072, 4096], P(('ctx', 'head')), may hold values from -8 to 8
- key: bfloat16 [3072, 2048], P(('ctx', 'head')), may hold values from -8 to 8
- value: bfloat16 [3072, 2048], P(('ctx', 'head')), may hold values from -8 to 8
- block_order: int32 [8], replicated, may hold values from 0 to 7, each once
Outputs:
- attended: bfloat16 [3072, 4096], P('ctx', 'head')
Inputs may be any that keep to these rules, and one draw needn't show every extreme that they name: `block_order`: each storage block index 0 to 7 appears exactly once.
All inputs are finite; a program needn't handle non-finite values.
Results may differ from a plain program's by a relative error of at most 0.0049.
Values may be sent and summed in bfloat16 or wider, within the bound.
A program may use at most 128 MiB of HBM per device.

v0:
```python
import jax
import jax.numpy as jnp
from jax import lax
from jax.sharding import PartitionSpec as P

HEAD_WIDTH = 128


query_scale = 1.0 / 12.0
softcap_limit = 50.0


def from_behind(value, axis, by):
    size = lax.axis_size(axis)
    return lax.ppermute(value, axis, [(i, (i + by) % size) for i in range(size)])


def block_pos(block_order, which_block, block_len):
    first = lax.dynamic_index_in_dim(block_order, which_block, 0, keepdims=False)
    return first * block_len + lax.iota(jnp.int32, block_len)


def add_block(totals, query_rows, query_pos, key_block, value_block, key_pos):
    numerator, denominator = totals
    scores = (
        jnp.einsum("rhgd,khd->hgrk", query_rows, key_block, preferred_element_type=jnp.float32)
        * query_scale
    )
    capped = softcap_limit * jnp.tanh(scores / softcap_limit)
    visible = key_pos[None, :] <= query_pos[:, None]
    weights = jnp.where(visible[None, None], jnp.exp(capped), jnp.zeros_like(capped))
    denominator = denominator + jnp.sum(weights, axis=-1)
    numerator = numerator + jnp.einsum(
        "hgrk,khd->rhgd",
        weights.astype(jnp.bfloat16),
        value_block,
        preferred_element_type=jnp.float32,
    )
    return (numerator, denominator)


def shards(query, key, value, block_order):
    query, key, value = (
        lax.all_to_all(query, "head", split_axis=1, concat_axis=0, tiled=True),
        lax.all_to_all(key, "head", split_axis=1, concat_axis=0, tiled=True),
        lax.all_to_all(value, "head", split_axis=1, concat_axis=0, tiled=True),
    )
    row_count = query.shape[0]
    block_len = row_count // 2
    kv_heads = key.shape[1] // HEAD_WIDTH
    group_size = query.shape[1] // key.shape[1]
    query_rows = query.reshape(row_count, kv_heads, group_size, HEAD_WIDTH)
    kv_pair = jnp.stack(
        [
            key.reshape(row_count, kv_heads, HEAD_WIDTH),
            value.reshape(row_count, kv_heads, HEAD_WIDTH),
        ]
    )
    cycle_size = lax.axis_size("ctx")
    cycle_index = lax.axis_index("ctx")
    query_pos = jnp.concatenate(
        [
            block_pos(block_order, 2 * cycle_index, block_len),
            block_pos(block_order, 2 * cycle_index + 1, block_len),
        ]
    )
    start_totals = (
        jnp.zeros((row_count, kv_heads, group_size, HEAD_WIDTH), jnp.float32),
        jnp.zeros((kv_heads, group_size, row_count), jnp.float32),
    )

    def add_shard(totals, held, source):
        for which_half in range(2):
            lower = which_half * block_len
            key_pos = block_pos(block_order, 2 * source + which_half, block_len)
            totals = add_block(
                totals,
                query_rows,
                query_pos,
                held[0, lower : lower + block_len],
                held[1, lower : lower + block_len],
                key_pos,
            )
        return totals

    totals = add_shard(start_totals, kv_pair, cycle_index)

    def from_lower(held):
        return from_behind(held, "ctx", 1)

    def turn_both(turn_index, state):
        forward_kv, backward_kv, sums = state
        forward_kv = from_lower(forward_kv)
        backward_kv = from_behind(backward_kv, "ctx", -1)
        sums = add_shard(sums, forward_kv, (cycle_index - turn_index) % cycle_size)
        sums = add_shard(sums, backward_kv, (cycle_index + turn_index) % cycle_size)
        return (forward_kv, backward_kv, sums)

    forward_kv, backward_kv, totals = lax.fori_loop(
        1, cycle_size // 2, turn_both, (kv_pair, kv_pair, totals)
    )
    forward_kv = from_lower(forward_kv)
    totals = add_shard(totals, forward_kv, (cycle_index + cycle_size // 2) % cycle_size)
    numerator, denominator = totals
    result = numerator / jnp.transpose(denominator, (2, 0, 1))[..., None]
    return result.reshape(row_count, kv_heads * group_size * HEAD_WIDTH).astype(jnp.bfloat16)


def solution(mesh):
    placed = (P(("ctx", "head"), None), P(("ctx", "head"), None), P(("ctx", "head"), None), P())
    return jax.shard_map(
        shards, mesh=mesh, in_specs=placed, out_specs=P("ctx", "head"), check_vma=False
    )
```

profile of v0, /device:TPU:1, one launch (start us, length us, event | category | flops | bytes accessed | tf_op | source)
XLA Modules:
  0.0 99.2 jit_solution(4919566508490505928)
XLA Ops:
  0.0 1.8 %copy.134 = bf16[12,8,8,256]{3,2,0,1:T(8,128)(2,1)} copy(bf16[12,8,8,256]{3,2,1,0:T(8,128)(2,1)} %bitcast.235) | data formatting | bytes 786432 | tf_op jit(solution)/shard_map/all_to_all | solution.py:45
  1.8 6.4 %all-to-all-start = ((bf16[96,8,256]{2,0,1:T(8,128)(2,1)}), bf16[96,8,256]{2,0,1:T(8,128)(2,1)S(1)}, u32[]{:S(2)}, u32[]{:S(2)}) async-start(bf16[96,8,256]{2,0,1:T(8,128)(2,1)} %bitcast.228), calls=%async_computation | async-start | bytes 786432 | tf_op jit(solution)/shard_map/all_to_all | solution.py:45
  8.1 1.8 %copy.135 = bf16[12,8,8,256]{3,2,0,1:T(8,128)(2,1)} copy(bf16[12,8,8,256]{3,2,1,0:T(8,128)(2,1)} %bitcast.236) | data formatting | bytes 786432 | tf_op jit(solution)/shard_map/all_to_all | solution.py:46
  9.9 7.4 %all-to-all-done = bf16[96,8,256]{2,0,1:T(8,128)(2,1)S(1)} async-done(((bf16[96,8,256]{2,0,1:T(8,128)(2,1)}), bf16[96,8,256]{2,0,1:T(8,128)(2,1)S(1)}, u32[]{:S(2)}, u32[]{:S(2)}) %all-to-all-start) | async-done | bytes 393248 | tf_op jit(solution)/shard_map/all_to_all | solution.py:45
  17.3 6.1 %all-to-all-start.2 = ((bf16[96,8,256]{2,0,1:T(8,128)(2,1)}), bf16[96,8,256]{2,0,1:T(8,128)(2,1)S(1)}, u32[]{:S(2)}, u32[]{:S(2)}) async-start(bf16[96,8,256]{2,0,1:T(8,128)(2,1)} %bitcast.229), calls=%async_computation.2 | async-start | bytes 786432 | tf_op jit(solution)/shard_map/all_to_all | solution.py:46
  23.4 1.6 %fusion.88 = (s32[1]{0:T(128)}, s32[1]{0:T(128)}, s32[1]{0:T(128)}, s32[1]{0:T(128)}, s32[1]{0:T(128)}, /*index=5*/s32[1]{0:T(128)}, s32[1]{0:T(128)}, s32[1]{0:T(128)}) fusion(s32[8]{0:T(128)} %param.7, s32[]{:T(128)S(6)} %select_n.95, s32[]{:T(128)S(6)} %select_n.90, s32[]{:T(128)S(6)} %select_n.88, s32[]{:T(128)S(6)} %select_n.85, s32[]{:T(128)S(6)} %select_n.83, ...), kind=kLoop, calls=%fused_computation.129 | loop fusion | bytes 96 | tf_op jit(solution)/shard_map/jit(dynamic_index_in_dim)/dynamic_slice | solution.py:19
  28.8 2.1 %copy.133 = bf16[12,8,8,512]{3,2,0,1:T(8,128)(2,1)} copy(bf16[12,8,8,512]{3,2,1,0:T(8,128)(2,1)} %bitcast.234) | data formatting | bytes 1572864 | tf_op jit(solution)/shard_map/all_to_all | solution.py:44
  30.9 1.6 %all-to-all-done.2 = bf16[96,8,256]{2,0,1:T(8,128)(2,1)S(1)} async-done(((bf16[96,8,256]{2,0,1:T(8,128)(2,1)}), bf16[96,8,256]{2,0,1:T(8,128)(2,1)S(1)}, u32[]{:S(2)}, u32[]{:S(2)}) %all-to-all-start.2) | async-done | bytes 393248 | tf_op jit(solution)/shard_map/all_to_all | solution.py:46
  32.5 6.1 %all-to-all-start.1 = ((bf16[96,8,512]{2,0,1:T(8,128)(2,1)}), bf16[96,8,512]{2,0,1:T(8,128)(2,1)S(1)}, u32[]{:S(2)}, u32[]{:S(2)}) async-start(bf16[96,8,512]{2,0,1:T(8,128)(2,1)} %bitcast.227), calls=%async_computation.1 | async-start | bytes 1572864 | tf_op jit(solution)/shard_map/all_to_all | solution.py:44
  39.8 2.4 %broadcast_compare_fusion = (pred[768,384]{0,1:T(8,128)(4,1)S(1)}, pred[768,384]{0,1:T(8,128)(4,1)}, pred[768,384]{0,1:T(8,128)(4,1)S(1)}, pred[768,384]{0,1:T(8...) fusion(s32[768]{0:T(1024)S(1)} %pad_add_fusion, ...), kind=kLoop, calls=%fused_computation.49 | loop fusion | flops 2359296 | bytes 2374656 | tf_op jit(solution)/shard_map/le | solution.py:30
  42.2 0.1 stack_reshape.6
  42.3 0.1 stack_reshape.7
  42.4 0.9 fusion.87
  43.2 0.8 copy_dynamic-update-slice_fusion
  44.0 2.2 %collective-permute-start = (bf16[2,768,2,128]{3,1,2,0:T(8,128)(2,1)}, bf16[2,768,2,128]{3,1,2,0:T(8,128)(2,1)}, u32[]{:S(2)}, u32[]{:S(2)}) collective-permute-start(bf16[2,768,2,128]{3,1,2,0:T(8,128)(2,1)} %copy_dynamic-update-slice_fusion), channel_id=1, source_target_pairs={{0,1},{1,2},{2,3},{3,0},{4,5},{5,6},{6,7},{7,4},{8,9},{9,10},{10,1... | collective-permute-start | bytes 2359304 | tf_op jit(solution)/shard_map/while/body/eval_jaxpr/ppermute | solution.py:15
  46.3 0.0 collective-permute-start.1
  46.3 0.3 fusion.86
  46.5 0.2 copy.90
  46.7 0.2 copy.91
  46.9 10.7 %all-to-all-done.1 = bf16[96,8,512]{2,0,1:T(8,128)(2,1)S(1)} async-done(((bf16[96,8,512]{2,0,1:T(8,128)(2,1)}), bf16[96,8,512]{2,0,1:T(8,128)(2,1)S(1)}, u32[]{:S(2)}, u32[]{:S(2)}) %all-to-all-start.1) | async-done | bytes 786464 | tf_op jit(solution)/shard_map/all_to_all | solution.py:44
  57.6 0.2 reshape.260
  57.8 0.0 copy-start.3
  57.8 2.8 %fusion = (f32[2,2,768]{2,1,0:T(2,128)S(1)}, f32[2,384,768,2]{2,1,3,0:T(8,128)S(1)}) fusion(pred[768,384]{0,1:T(8,128)(4,1)} %get-tuple-element.46, bf16[768,2,2,128]{3,2,1,0:T(2,128)(2,1)S(1)} %reshape.260, bf16[1,768,2,128]{3,1,2,0:T(8,128)(2,1)S(1)} %get-tuple-element.25), kind=kOutput, calls=%fused_computation.8 | convolution fusion | flops 306705408 | bytes 6008832 | tf_op jit(solution)/shard_map/rhgd,khd->hgrk/dot_general | solution.py:26
  60.6 0.0 copy-start.2
  60.6 0.0 copy-done.3
  60.6 1.8 %fusion.30 = f32[2,2,768,128]{2,3,1,0:T(8,128)S(1)} fusion(f32[2,384,768,2]{2,1,3,0:T(8,128)S(1)} %get-tuple-element.68, pred[768,384]{0,1:T(8,128)(4,1)S(1)} %copy-done.3, bf16[1,384,2,128]{1,3,2,0:T(8,128)(2,1)S(1)} %copy.90), kind=kOutput, calls=%fused_computation.31 | convolution fusion | flops 306708480 | bytes 6782976 | tf_op jit(solution)/shard_map/hgrk,khd->rhgd/dot_general | solution.py:33
  62.4 0.0 copy-done.2
  62.4 1.8 %fusion.2 = (f32[2,2,768]{2,1,0:T(2,128)S(1)}, f32[2,384,768,2]{2,1,3,0:T(8,128)S(1)}) fusion(pred[768,384]{0,1:T(8,128)(4,1)S(1)} %copy-done.2, bf16[768,2,2,128]{3,2,1,0:T(2,128)(2,1)S(1)} %reshape.260, bf16[1,768,2,128]{3,1,2,0:T(8,128)(2,1)S(1)} %get-tuple-element.25), kind=kOutput, calls=%fused_computation.10 | convolution fusion | flops 306705408 | bytes 6008832 | tf_op jit(solution)/shard_map/rhgd,khd->hgrk/dot_general | solution.py:26
  64.2 1.8 %fusion.28 = f32[2,2,768,128]{2,3,1,0:T(8,128)S(1)} fusion(f32[2,384,768,2]{2,1,3,0:T(8,128)S(1)} %get-tuple-element.70, pred[768,384]{0,1:T(8,128)(4,1)S(1)} %copy-done.2, bf16[1,384,2,128]{1,3,2,0:T(8,128)(2,1)S(1)} %copy.91), kind=kOutput, calls=%fused_computation.30 | convolution fusion | flops 306708480 | bytes 6782976 | tf_op jit(solution)/shard_map/hgrk,khd->rhgd/dot_general | solution.py:33
  66.0 0.0 collective-permute-done
  66.0 3.5 %collective-permute-start.2 = (bf16[2,768,2,128]{3,1,2,0:T(8,128)(2,1)}, bf16[2,768,2,128]{3,1,2,0:T(8,128)(2,1)S(1)}, u32[]{:S(2)}, u32[]{:S(2)}) collective-permute-start(bf16[2,768,2,128]{3,1,2,0:T(8,128)(2,1)} %collective-permute-done), channel_id=1, source_target_pairs={{0,1},{1,2},{2,3},{3,0},{4,5},{5,6},{6,7},{7,4},{8,9},{9,10},{10,1... | collective-permute-start | bytes 2359304 | tf_op jit(solution)/shard_map/ppermute | solution.py:15
  69.5 0.0 collective-permute-done.1
  69.5 0.0 copy-done.1
  69.5 2.7 %fusion.10 = (f32[2,2,768]{2,1,0:T(2,128)S(1)}, f32[2,384,768,2]{2,1,3,0:T(8,128)S(1)}) fusion(pred[768,384]{0,1:T(8,128)(4,1)S(1)} %copy-done.1, bf16[768,2,2,128]{3,2,1,0:T(2,128)(2,1)S(1)} %reshape.260, bf16[2,768,2,128]{3,1,2,0:T(8,128)(2,1)} %collective-permute-done.1), kind=kOutput, calls=%fused_computation.18 | convolution fusion | flops 306705408 | bytes 6008832 | tf_op jit(solution)/shard_map/while/body/eval_jaxpr/rhgd,khd->hgrk/dot_general | solution.py:26
  72.2 2.6 %fusion.20 = f32[2,128,2,768]{3,1,2,0:T(8,128)S(1)} fusion(f32[2,384,768,2]{2,1,3,0:T(8,128)S(1)} %get-tuple-element.60, pred[768,384]{0,1:T(8,128)(4,1)S(1)} %copy-done.1, bf16[2,768,2,128]{3,1,2,0:T(8,128)(2,1)} %collective-permute-done.1), kind=kOutput, calls=%fused_computation.26 | convolution fusion | flops 306708480 | bytes 6782976 | tf_op jit(solution)/shard_map/while/body/eval_jaxpr/hgrk,khd->rhgd/dot_general | solution.py:33
  74.8 0.0 copy-done
  74.8 2.7 %fusion.8 = (f32[2,2,768]{2,1,0:T(2,128)S(1)}, f32[2,384,768,2]{2,1,3,0:T(8,128)S(1)}) fusion(pred[768,384]{0,1:T(8,128)(4,1)S(1)} %copy-done, bf16[768,2,2,128]{3,2,1,0:T(2,128)(2,1)S(1)} %reshape.260, bf16[2,768,2,128]{3,1,2,0:T(8,128)(2,1)} %collective-permute-done.1), kind=kOutput, calls=%fused_computation.16 | convolution fusion | flops 306705408 | bytes 6008832 | tf_op jit(solution)/shard_map/while/body/eval_jaxpr/rhgd,khd->hgrk/dot_general | solution.py:26
  77.5 2.5 %fusion.22 = f32[2,128,2,768]{3,1,2,0:T(8,128)S(1)} fusion(f32[2,384,768,2]{2,1,3,0:T(8,128)S(1)} %get-tuple-element.62, pred[768,384]{0,1:T(8,128)(4,1)S(1)} %copy-done, bf16[2,768,2,128]{3,1,2,0:T(8,128)(2,1)} %collective-permute-done.1), kind=kOutput, calls=%fused_computation.27 | convolution fusion | flops 306708480 | bytes 6782976 | tf_op jit(solution)/shard_map/while/body/eval_jaxpr/hgrk,khd->rhgd/dot_general | solution.py:33
  80.1 2.7 %fusion.6 = (f32[2,2,768]{2,1,0:T(2,128)S(1)}, f32[2,384,768,2]{2,1,3,0:T(8,128)S(1)}) fusion(pred[768,384]{0,1:T(8,128)(4,1)S(1)} %get-tuple-element.40, bf16[768,2,2,128]{3,2,1,0:T(2,128)(2,1)S(1)} %reshape.260, bf16[2,768,2,128]{3,1,2,0:T(8,128)(2,1)} %collective-permute-done), kind=kOutput, calls=%fused_computation.14 | convolution fusion | flops 306705408 | bytes 6008832 | tf_op jit(solution)/shard_map/while/body/eval_jaxpr/rhgd,khd->hgrk/dot_general | solution.py:26
  82.8 2.5 %fusion.24 = f32[2,128,2,768]{3,1,2,0:T(8,128)S(1)} fusion(f32[2,384,768,2]{2,1,3,0:T(8,128)S(1)} %get-tuple-element.64, pred[768,384]{0,1:T(8,128)(4,1)S(1)} %get-tuple-element.40, bf16[2,768,2,128]{3,1,2,0:T(8,128)(2,1)} %collective-permute-done), kind=kOutput, calls=%fused_computation.28 | convolution fusion | flops 306708480 | bytes 6782976 | tf_op jit(solution)/shard_map/while/body/eval_jaxpr/hgrk,khd->rhgd/dot_general | solution.py:33
  85.3 2.7 %fusion.4 = (f32[2,2,768]{2,1,0:T(2,128)S(1)}, f32[2,384,768,2]{2,1,3,0:T(8,128)S(1)}) fusion(pred[768,384]{0,1:T(8,128)(4,1)S(1)} %get-tuple-element.29, bf16[768,2,2,128]{3,2,1,0:T(2,128)(2,1)S(1)} %reshape.260, bf16[2,768,2,128]{3,1,2,0:T(8,128)(2,1)} %collective-permute-done), kind=kOutput, calls=%fused_computation.12 | convolution fusion | flops 306705408 | bytes 6008832 | tf_op jit(solution)/shard_map/while/body/eval_jaxpr/rhgd,khd->hgrk/dot_general | solution.py:26
  88.1 2.7 %fusion.26 = f32[2,128,2,768]{3,1,2,0:T(8,128)S(1)} fusion(f32[2,384,768,2]{2,1,3,0:T(8,128)S(1)} %get-tuple-element.66, pred[768,384]{0,1:T(8,128)(4,1)S(1)} %get-tuple-element.29, bf16[2,768,2,128]{3,1,2,0:T(8,128)(2,1)} %collective-permute-done), kind=kOutput, calls=%fused_computation.29 | convolution fusion | flops 306708480 | bytes 6782976 | tf_op jit(solution)/shard_map/while/body/eval_jaxpr/hgrk,khd->rhgd/dot_general | solution.py:33
  90.8 0.0 collective-permute-done.2
  90.8 1.8 %fusion.12 = (f32[2,2,768]{2,1,0:T(2,128)S(1)}, f32[2,384,768,2]{2,1,3,0:T(8,128)S(1)}) fusion(pred[768,384]{0,1:T(8,128)(4,1)S(1)} %get-tuple-element.45, bf16[768,2,2,128]{3,2,1,0:T(2,128)(2,1)S(1)} %reshape.260, bf16[2,768,2,128]{3,1,2,0:T(8,128)(2,1)S(1)} %collective-permute-done.2), kind=kOutput, calls=%fused_computation.20 | convolution fusion | flops 306705408 | bytes 6008832 | tf_op jit(solution)/shard_map/rhgd,khd->hgrk/dot_general | solution.py:26
  92.6 1.8 %fusion.14 = (f32[2,2,768]{2,1,0:T(2,128)S(1)}, f32[2,384,768,2]{2,1,3,0:T(8,128)S(1)}) fusion(pred[768,384]{0,1:T(8,128)(4,1)S(1)} %get-tuple-element.27, bf16[768,2,2,128]{3,2,1,0:T(2,128)(2,1)S(1)} %reshape.260, bf16[2,768,2,128]{3,1,2,0:T(8,128)(2,1)S(1)} %collective-permute-done.2), kind=kOutput, calls=%fused_computation.22 | convolution fusion | flops 306705408 | bytes 6008832 | tf_op jit(solution)/shard_map/rhgd,khd->hgrk/dot_general | solution.py:26
  94.4 1.6 %fusion.18 = f32[2,128,2,768]{3,1,2,0:T(8,128)S(1)} fusion(f32[2,384,768,2]{2,1,3,0:T(8,128)S(1)} %get-tuple-element.58, pred[768,384]{0,1:T(8,128)(4,1)S(1)} %get-tuple-element.45, bf16[2,768,2,128]{3,1,2,0:T(8,128)(2,1)S(1)} %collective-permute-done.2), kind=kOutput, calls=%fused_computation.25 | convolution fusion | flops 306708480 | bytes 6782976 | tf_op jit(solution)/shard_map/hgrk,khd->rhgd/dot_general | solution.py:33
  96.1 2.0 %fusion.41 = bf16[768,2,2,128]{0,3,2,1:T(8,128)(2,1)S(1)} fusion(f32[2,128,2,768]{3,1,2,0:T(8,128)S(1)} %fusion.18, f32[2,128,2,768]{3,1,2,0:T(8,128)S(1)} %fusion.20, f32[2,128,2,768]{3,1,2,0:T(8,128)S(1)} %fusion.22, f32[2,128,2,768]{3,1,2,0:T(8,128)S(1)} %fusion.24, f32[2,128,2,768]{3,1,2,0:T(8,128)S(1)} %fusion.26, f32[2,2,768,128]{2,3,1,0:T(8,128)S(1)} %fusion.30, ...), kind=kOutput, calls=%fused_computation.42 | convolution fusion | flops 310247424 | bytes 17018880 | tf_op jit(solution)/shard_map/hgrk,khd->rhgd/dot_general | solution.py:33
  98.1 1.2 %copy.53 = bf16[768,512]{1,0:T(8,128)(2,1)} copy(bf16[768,512]{0,1:T(8,128)(2,1)S(1)} %bitcast.230) | data formatting | bytes 1572864 | tf_op jit(solution)/shard_map/convert_element_type | solution.py:106
  (8 shorter events, 0.1 us)
Async XLA Ops:
  1.8 15.5 %all-to-all-start = ((bf16[96,8,256]{2,0,1:T(8,128)(2,1)}), bf16[96,8,256]{2,0,1:T(8,128)(2,1)S(1)}, u32[]{:S(2)}, u32[]{:S(2)}) async-start(bf16[96,8,256]{2,0,1:T(8,128)(2,1)} %bitcast.228), calls=%async_computation | async-start | bytes 786432 | tf_op jit(solution)/shard_map/all_to_all | solution.py:45
  17.3 15.2 %all-to-all-start.2 = ((bf16[96,8,256]{2,0,1:T(8,128)(2,1)}), bf16[96,8,256]{2,0,1:T(8,128)(2,1)S(1)}, u32[]{:S(2)}, u32[]{:S(2)}) async-start(bf16[96,8,256]{2,0,1:T(8,128)(2,1)} %bitcast.229), calls=%async_computation.2 | async-start | bytes 786432 | tf_op jit(solution)/shard_map/all_to_all | solution.py:46
  32.5 25.1 %all-to-all-start.1 = ((bf16[96,8,512]{2,0,1:T(8,128)(2,1)}), bf16[96,8,512]{2,0,1:T(8,128)(2,1)S(1)}, u32[]{:S(2)}, u32[]{:S(2)}) async-start(bf16[96,8,512]{2,0,1:T(8,128)(2,1)} %bitcast.227), calls=%async_computation.1 | async-start | bytes 1572864 | tf_op jit(solution)/shard_map/all_to_all | solution.py:44
  44.0 22.0 %collective-permute-start = (bf16[2,768,2,128]{3,1,2,0:T(8,128)(2,1)}, bf16[2,768,2,128]{3,1,2,0:T(8,128)(2,1)}, u32[]{:S(2)}, u32[]{:S(2)}) collective-permute-start(bf16[2,768,2,128]{3,1,2,0:T(8,128)(2,1)} %copy_dynamic-update-slice_fusion), channel_id=1, source_target_pairs={{0,1},{1,2},{2,3},{3,0},{4,5},{5,6},{6,7},{7,4},{8,9},{9,10},{10,1... | collective-permute-start | bytes 2359304 | tf_op jit(solution)/shard_map/while/body/eval_jaxpr/ppermute | solution.py:15
  46.3 23.2 %collective-permute-start.1 = (bf16[2,768,2,128]{3,1,2,0:T(8,128)(2,1)}, bf16[2,768,2,128]{3,1,2,0:T(8,128)(2,1)}, u32[]{:S(2)}, u32[]{:S(2)}) collective-permute-start(bf16[2,768,2,128]{3,1,2,0:T(8,128)(2,1)} %copy_dynamic-update-slice_fusion), channel_id=1, source_target_pairs={{0,3},{1,0},{2,1},{3,2},{4,7},{5,4},{6,5},{7,6},{8,11},{9,8},{10,9... | collective-permute-start | bytes 2359304 | tf_op jit(solution)/shard_map/while/body/eval_jaxpr/ppermute | solution.py:15
  57.8 2.8 %copy-start.3 = (pred[768,384]{0,1:T(8,128)(4,1)S(1)}, pred[768,384]{0,1:T(8,128)(4,1)}, u32[]{:S(2)}) copy-start(pred[768,384]{0,1:T(8,128)(4,1)} %get-tuple-element.46) | copy-start | bytes 884740
  60.6 1.8 %copy-start.2 = (pred[768,384]{0,1:T(8,128)(4,1)S(1)}, pred[768,384]{0,1:T(8,128)(4,1)}, u32[]{:S(2)}) copy-start(pred[768,384]{0,1:T(8,128)(4,1)} %get-tuple-element.28) | copy-start | bytes 884740
  64.2 5.3 %copy-start.1 = (pred[768,384]{0,1:T(8,128)(4,1)S(1)}, pred[768,384]{0,1:T(8,128)(4,1)}, u32[]{:S(2)}) copy-start(pred[768,384]{0,1:T(8,128)(4,1)} %get-tuple-element.44) | copy-start | bytes 884740
  66.0 24.8 %collective-permute-start.2 = (bf16[2,768,2,128]{3,1,2,0:T(8,128)(2,1)}, bf16[2,768,2,128]{3,1,2,0:T(8,128)(2,1)S(1)}, u32[]{:S(2)}, u32[]{:S(2)}) collective-permute-start(bf16[2,768,2,128]{3,1,2,0:T(8,128)(2,1)} %collective-permute-done), channel_id=1, source_target_pairs={{0,1},{1,2},{2,3},{3,0},{4,5},{5,6},{6,7},{7,4},{8,9},{9,10},{10,1... | collective-permute-start | bytes 2359304 | tf_op jit(solution)/shard_map/ppermute | solution.py:15
  72.2 2.6 %copy-start = (pred[768,384]{0,1:T(8,128)(4,1)S(1)}, pred[768,384]{0,1:T(8,128)(4,1)}, u32[]{:S(2)}) copy-start(pred[768,384]{0,1:T(8,128)(4,1)} %get-tuple-element.42) | copy-start | bytes 884740
where the time goes:
time: 100 us; the launch traced here: 99.2 us
  matrix products  36.6 us (37%)
  starting transfers between devices  24.2 us (24%)
  waiting for transfers between devices  19.7 us (20%)
  local copies, waits for them, and re-layouts  11.1 us (11%)
  between operations  5.27 us (5%)
  other arithmetic  2.43 us (2%)
    dot_general x8, matrix products, add_block(): jnp.einsum('rhgd,khd->hgrk', query_rows, key_block, preferred_element_typ...  19 us
    dot_general x8, matrix products, add_block(): jnp.einsum('hgrk,khd->rhgd', weights.astype(jnp.bfloat16), value_block, p...  17.6 us
    all_to_all x1, waiting for transfers between devices, shards(): lax.all_to_all(query, 'head', split_axis=1, concat_axis=0, tiled=True)  10.7 us
    all_to_all x1, waiting for transfers between devices, shards(): lax.all_to_all(key, 'head', split_axis=1, concat_axis=0, tiled=True)  7.41 us
    all_to_all x1, starting transfers between devices, shards(): lax.all_to_all(key, 'head', split_axis=1, concat_axis=0, tiled=True)  6.37 us
    all_to_all x1, starting transfers between devices, shards(): lax.all_to_all(query, 'head', split_axis=1, concat_axis=0, tiled=True)  6.06 us
    all_to_all x1, starting transfers between devices, shards(): lax.all_to_all(value, 'head', split_axis=1, concat_axis=0, tiled=True)  6.06 us
    ppermute x3, starting transfers between devices, from_behind(): lax.ppermute(value, axis, [(i, (i + by) % size) for i in range(size)])  5.67 us
  transfers between devices with their start and end apart: 6, of which 3 were waited for; matrix products, arithmetic and copies ran while one was open for 40% of the time, Pallas kernels for 0%

commit v1 on v0

v1 whole, which is shorter than its diff:
```python
import functools
import math

import jax
import jax.numpy as jnp
from jax import lax
from jax.experimental import pallas as pl
from jax.experimental.pallas import tpu as pltpu
from jax.sharding import PartitionSpec as P

HEAD_WIDTH = 128
MESH = pl.DeviceIdType.MESH
CAP = 50.0
IN_SCALE = 1.0 / (12.0 * CAP)
OUT_SCALE = CAP * math.log2(math.e)
HIDDEN = -4096.0


def flip(index, step, size):
    out, bit = 0, 1
    while bit < size:
        mine = (index // bit) % 2
        turn = (step // bit) % 2
        out = out + (mine + turn - 2 * mine * turn) * bit
        bit *= 2
    return out


def kernel(
    n_head, n_ctx, pair,
    order, query, key, value, out,
    qbuf, kv, acc,
    q_send, k_send, v_send, q_recv, k_recv, v_recv,
    local_sem, f_send, r_send, f_recv,
):
    me = lax.axis_index("head")
    ctx = lax.axis_index("ctx")
    chip, core = ctx // 2, ctx % 2
    partner = chip * 2 + 1 - core
    chips = n_ctx // 2
    pieces = n_head // pair
    rows = query.shape[0]
    total = rows * n_head
    block = total // 2
    q_cols = query.shape[1] // n_head
    kv_cols = key.shape[1] // n_head
    kv_heads = kv_cols // HEAD_WIDTH
    per_kv = q_cols // kv_cols
    piece_rows = rows * pair
    same_core = [((chip + t) % chips) * 2 + core for t in range(1, chips)]
    peers = [flip(me, j, n_head) for j in range(1, n_head)]

    barrier = pltpu.get_barrier_semaphore()
    for d in peers:
        pl.semaphore_signal(barrier, inc=1, device_id={"head": d}, device_id_type=MESH)
    for c in [partner] + same_core:
        pl.semaphore_signal(barrier, inc=1, device_id={"ctx": c}, device_id_type=MESH)

    def rows_of(s):
        return pl.ds(pl.multiple_of(s * rows, rows), rows)

    def cols_of(s, width):
        return pl.ds(pl.multiple_of(s * width, width), width)

    mine = [
        pltpu.make_async_copy(key.at[:, cols_of(me, kv_cols)], kv.at[ctx, 0, rows_of(me)], local_sem.at[0]),
        pltpu.make_async_copy(value.at[:, cols_of(me, kv_cols)], kv.at[ctx, 1, rows_of(me)], local_sem.at[1]),
        pltpu.make_async_copy(query.at[:, cols_of(me, q_cols)], qbuf.at[rows_of(me)], local_sem.at[2]),
    ]
    for copy in mine:
        copy.start()

    pl.semaphore_wait(barrier, n_head - 1 + chips)

    def to_head(src, width, dst, send, recv, d):
        return pltpu.make_async_remote_copy(
            src_ref=src.at[:, cols_of(d, width)], dst_ref=dst.at[rows_of(me)],
            send_sem=send.at[d], recv_sem=recv.at[me],
            device_id={"head": d}, device_id_type=MESH,
        )

    sends = []
    for d in peers:
        sends.append(to_head(key, kv_cols, kv.at[ctx, 0], k_send, k_recv, d))
        sends.append(to_head(value, kv_cols, kv.at[ctx, 1], v_send, v_recv, d))
    for d in peers:
        sends.append(to_head(query, q_cols, qbuf, q_send, q_recv, d))
    for copy in sends:
        copy.start()

    def arrived(dst, recv, s):
        pltpu.make_async_copy(dst.at[rows_of(s)], dst.at[rows_of(s)], recv.at[s]).wait()

    def piece_ref(c, p):
        return kv.at[c, :, pl.ds(pl.multiple_of(p * piece_rows, piece_rows), piece_rows)]

    def forward(c, p, dest, send):
        return pltpu.make_async_remote_copy(
            src_ref=piece_ref(c, p), dst_ref=piece_ref(c, p),
            send_sem=send, recv_sem=f_recv.at[c, p],
            device_id={"ctx": dest}, device_id_type=MESH,
        )

    def piece_arrived(c, p):
        pltpu.make_async_copy(piece_ref(c, p), piece_ref(c, p), f_recv.at[c, p]).wait()

    passed = []

    def relay(p):
        for c in same_core:
            piece_arrived(c, p)
            copy = forward(c, p, partner, r_send.at[c, p])
            copy.start()
            passed.append(copy)

    home = me // pair
    for step in range(pieces):
        p = flip(home, step, pieces)
        for t in range(pair):
            s = flip(me, step * pair + t, n_head)
            if step == 0 and t == 0:
                mine[0].wait()
                mine[1].wait()
            else:
                arrived(kv.at[ctx, 0], k_recv, s)
                arrived(kv.at[ctx, 1], v_recv, s)
        for dest in same_core + [partner]:
            copy = forward(ctx, p, dest, f_send.at[dest, p])
            copy.start()
            passed.append(copy)
        if step > 0:
            relay(flip(home, step - 1, pieces))
    relay(flip(home, pieces - 1, pieces))
    for t in range(chips):
        c = ((chip + t) % chips) * 2 + 1 - core
        for step in range(pieces):
            piece_arrived(c, flip(home, step, pieces))
    mine[2].wait()

    ones = jnp.ones((total, HEAD_WIDTH), jnp.bfloat16)

    def q_head(g, h):
        span = pl.ds(pl.multiple_of(g * piece_rows, piece_rows), piece_rows)
        return jnp.concatenate(
            [qbuf[span, (h * per_kv + i) * HEAD_WIDTH : (h * per_kv + i + 1) * HEAD_WIDTH] for i in range(per_kv)],
            axis=0,
        )

    def scores_of(g, h, c):
        k = kv[c, 0, :, h * HEAD_WIDTH : (h + 1) * HEAD_WIDTH]
        s = lax.dot_general(q_head(g, h), k, (((1,), (1,)), ((), ())), preferred_element_type=jnp.float32)
        return jnp.tanh(s * IN_SCALE) * OUT_SCALE

    def weighted(w, h, c):
        v = kv[c, 1, :, h * HEAD_WIDTH : (h + 1) * HEAD_WIDTH]
        return jnp.dot(w.astype(jnp.bfloat16), jnp.concatenate([v, ones], axis=1), preferred_element_type=jnp.float32)

    def one_group(step, carry):
        g = flip(home, step, pieces)
        for t in range(pair):
            j = step * pair + t
            s = flip(me, j, n_head)

            @pl.when(j > 0)
            def _():
                arrived(qbuf, q_recv, s)

        first_row = g * piece_rows
        half = first_row // block
        q_block = order[2 * ctx + half]
        q_pos = q_block * block + (first_row - half * block) + lax.broadcasted_iota(jnp.int32, (piece_rows, total), 0)
        col = lax.broadcasted_iota(jnp.int32, (piece_rows, total), 1)
        k_pos = jnp.where(col < block, order[2 * ctx] * block + col, order[2 * ctx + 1] * block + col - block)
        visible = k_pos <= q_pos
        for h in range(kv_heads):
            e = jnp.exp2(scores_of(g, h, ctx)).reshape(per_kv, piece_rows, total)
            w = jnp.where(visible[None], e, 0.0).reshape(per_kv * piece_rows, total)
            acc[h] = weighted(w, h, ctx)

        def other(d, carry):
            c = (ctx + d) % n_ctx
            low = jnp.where(order[2 * c] <= q_block, 0.0, HIDDEN)
            high = jnp.where(order[2 * c + 1] <= q_block, 0.0, HIDDEN)
            for h in range(kv_heads):
                x = scores_of(g, h, c)
                w = jnp.concatenate([jnp.exp2(x[:, :block] + low), jnp.exp2(x[:, block:] + high)], axis=1)
                acc[h] += weighted(w, h, c)
            return carry

        lax.fori_loop(1, n_ctx, other, 0)
        span = pl.ds(pl.multiple_of(first_row, piece_rows), piece_rows)
        for h in range(kv_heads):
            a = acc[h]
            o = (a[:, :HEAD_WIDTH] / a[:, HEAD_WIDTH:]).astype(jnp.bfloat16)
            for i in range(per_kv):
                at = (h * per_kv + i) * HEAD_WIDTH
                out[span, at : at + HEAD_WIDTH] = o[i * piece_rows : (i + 1) * piece_rows]
        return carry

    lax.fori_loop(0, pieces, one_group, 0)
    for copy in sends:
        copy.wait_send()
    for copy in passed:
        copy.wait_send()


def shards(n_head, n_ctx, query, key, value, block_order):
    rows = query.shape[0]
    total = rows * n_head
    q_cols = query.shape[1] // n_head
    kv_cols = key.shape[1] // n_head
    kv_heads = kv_cols // HEAD_WIDTH
    per_kv = q_cols // kv_cols
    pair = 2
    pieces = n_head // pair
    hbm = pl.BlockSpec(memory_space=pltpu.HBM)
    dma = pltpu.SemaphoreType.DMA
    return pl.pallas_call(
        functools.partial(kernel, n_head, n_ctx, pair),
        out_shape=jax.ShapeDtypeStruct((total, q_cols), jnp.bfloat16),
        in_specs=[pl.BlockSpec(memory_space=pltpu.SMEM), hbm, hbm, hbm],
        out_specs=pl.BlockSpec(memory_space=pltpu.VMEM),
        scratch_shapes=[
            pltpu.VMEM((total, q_cols), jnp.bfloat16),
            pltpu.VMEM((n_ctx, 2, total, kv_cols), jnp.bfloat16),
            pltpu.VMEM((kv_heads, per_kv * pair * rows, 2 * HEAD_WIDTH), jnp.float32),
            dma((n_head,)), dma((n_head,)), dma((n_head,)),
            dma((n_head,)), dma((n_head,)), dma((n_head,)),
            dma((3,)),
            dma((n_ctx, pieces)), dma((n_ctx, pieces)), dma((n_ctx, pieces)),
        ],
        compiler_params=pltpu.CompilerParams(
            collective_id=0, has_side_effects=True, vmem_limit_bytes=60 * 1024 * 1024
        ),
    )(block_order, query, key, value)


def solution(mesh):
    placed = (P(("ctx", "head"), None), P(("ctx", "head"), None), P(("ctx", "head"), None), P())
    return jax.shard_map(
        functools.partial(shards, mesh.shape["head"], mesh.shape["ctx"]),
        mesh=mesh, in_specs=placed, out_specs=P("ctx", "head"), check_vma=False,
    )
```

time: 100 us -> 57.5 us (0.57)
  the two profiles are of different devices: /device:TPU:1 before, /device:TPU:9 now
where the time goes in v1:
time: 57.5 us; the launch traced here: 57.4 us
  Pallas kernels  55.3 us (96%)
  local copies, waits for them, and re-layouts  2.06 us (4%)
    pallas_call x1, Pallas kernels, shards(): pl.pallas_call(functools.partial(kernel, n_head, n_ctx, pair), out_shape=...  55.3 us
    unnamed x1, local copies, waits for them, and re-layouts  2.06 us

profile of v1, /device:TPU:9, one launch (start us, length us, event | category | flops | bytes accessed | tf_op | source)
XLA Modules:
  0.0 57.4 jit_solution(12148787622512184905)
XLA Ops:
  0.0 55.3 %shard_map.46 = bf16[768,512]{1,0:T(8,128)(2,1)} custom-call(s32[8]{0:T(128)} %order.1, bf16[96,4096]{1,0:T(8,128)(2,1)} %query.1, bf16[96,2048]{1,0:T(8,128)(2,1)} %key.1, bf16[96,2048]{1,0:T(8,128)(2,1)} %value.1), custom_call_target="tpu_custom_call" | custom-call | tf_op jit(solution)/shard_map/pallas_call | solution.py:218
  55.3 2.1 %copy.6 = bf16[768,512]{1,0:T(8,128)(2,1)} copy(bf16[768,512]{1,0:T(8,128)(2,1)} %shard_map.46) | data formatting | bytes 1572864

commit v2 on v1

--- a/solution.py
+++ b/solution.py
@@ -79,12 +79,14 @@
             device_id={"head": d}, device_id_type=MESH,
         )
 
+    near = n_head // 2
     sends = []
-    for d in peers:
-        sends.append(to_head(key, kv_cols, kv.at[ctx, 0], k_send, k_recv, d))
-        sends.append(to_head(value, kv_cols, kv.at[ctx, 1], v_send, v_recv, d))
-    for d in peers:
-        sends.append(to_head(query, q_cols, qbuf, q_send, q_recv, d))
+    for some in (peers[: near - 1], peers[near - 1 :]):
+        for d in some:
+            sends.append(to_head(key, kv_cols, kv.at[ctx, 0], k_send, k_recv, d))
+            sends.append(to_head(value, kv_cols, kv.at[ctx, 1], v_send, v_recv, d))
+        for d in some:
+            sends.append(to_head(query, q_cols, qbuf, q_send, q_recv, d))
     for copy in sends:
         copy.start()
 
@@ -114,7 +116,10 @@
             passed.append(copy)
 
     home = me // pair
-    for step in range(pieces):
+    near_pieces = pieces // 2
+    near_half = home // near_pieces
+
+    def collect(step):
         p = flip(home, step, pieces)
         for t in range(pair):
             s = flip(me, step * pair + t, n_head)
@@ -128,76 +133,110 @@
             copy = forward(ctx, p, dest, f_send.at[dest, p])
             copy.start()
             passed.append(copy)
-        if step > 0:
-            relay(flip(home, step - 1, pieces))
-    relay(flip(home, pieces - 1, pieces))
-    for t in range(chips):
+
+    def others_arrived(t, steps):
         c = ((chip + t) % chips) * 2 + 1 - core
-        for step in range(pieces):
+        for step in steps:
             piece_arrived(c, flip(home, step, pieces))
-    mine[2].wait()
-
-    ones = jnp.ones((total, HEAD_WIDTH), jnp.bfloat16)
-
-    def q_head(g, h):
-        span = pl.ds(pl.multiple_of(g * piece_rows, piece_rows), piece_rows)
-        return jnp.concatenate(
-            [qbuf[span, (h * per_kv + i) * HEAD_WIDTH : (h * per_kv + i + 1) * HEAD_WIDTH] for i in range(per_kv)],
-            axis=0,
-        )
-
-    def scores_of(g, h, c):
-        k = kv[c, 0, :, h * HEAD_WIDTH : (h + 1) * HEAD_WIDTH]
-        s = lax.dot_general(q_head(g, h), k, (((1,), (1,)), ((), ())), preferred_element_type=jnp.float32)
-        return jnp.tanh(s * IN_SCALE) * OUT_SCALE
-
-    def weighted(w, h, c):
-        v = kv[c, 1, :, h * HEAD_WIDTH : (h + 1) * HEAD_WIDTH]
-        return jnp.dot(w.astype(jnp.bfloat16), jnp.concatenate([v, ones], axis=1), preferred_element_type=jnp.float32)
-
-    def one_group(step, carry):
+
+    ones = jnp.ones((2 * block, HEAD_WIDTH), jnp.bfloat16)
+
+    def unit(step, far, t, diagonal):
         g = flip(home, step, pieces)
+        first_row = g * piece_rows
+        q_half = first_row // block
+        q_block = order[2 * ctx + q_half]
+        half = near_half + far - 2 * near_half * far
+        c0 = ((chip + t) % chips) * 2 + core
+        c1 = ((chip + t) % chips) * 2 + 1 - core
+        q_span = pl.ds(pl.multiple_of(first_row, piece_rows), piece_rows)
+        k_span = pl.ds(pl.multiple_of(half * block, block), block)
+        low = jnp.where(order[2 * c0 + half] <= q_block, 0.0, HIDDEN)
+        high = jnp.where(order[2 * c1 + half] <= q_block, 0.0, HIDDEN)
+        for h in range(kv_heads):
+            cols = slice(h * HEAD_WIDTH, (h + 1) * HEAD_WIDTH)
+            q = jnp.concatenate(
+                [qbuf[q_span, (h * per_kv + i) * HEAD_WIDTH : (h * per_kv + i + 1) * HEAD_WIDTH] for i in range(per_kv)],
+                axis=0,
+            )
+            k = jnp.concatenate([kv[c0, 0, k_span, cols], kv[c1, 0, k_span, cols]], axis=0)
+            v = jnp.concatenate([kv[c0, 1, k_span, cols], kv[c1, 1, k_span, cols]], axis=0)
+            x = lax.dot_general(q, k, (((1,), (1,)), ((), ())), preferred_element_type=jnp.float32)
+            x = jnp.tanh(x * IN_SCALE) * OUT_SCALE
+            if diagonal:
+                q_at = first_row - q_half * block + lax.broadcasted_iota(jnp.int32, (piece_rows, block), 0)
+                visible = lax.broadcasted_iota(jnp.int32, (piece_rows, block), 1) <= q_at
+                e = jnp.exp2(x[:, :block]).reshape(per_kv, piece_rows, block)
+                left = jnp.where(visible[None], e, 0.0).reshape(per_kv * piece_rows, block)
+            else:
+                left = jnp.exp2(x[:, :block] + low)
+            w = jnp.concatenate([left, jnp.exp2(x[:, block:] + high)], axis=1).astype(jnp.bfloat16)
+            o = jnp.dot(w, jnp.concatenate([v, ones], axis=1), preferred_element_type=jnp.float32)
+            if diagonal:
+                acc[step, h] = o
+            else:
+                acc[step, h] += o
+
+    def q_arrived(step):
         for t in range(pair):
             j = step * pair + t
-            s = flip(me, j, n_head)
 
             @pl.when(j > 0)
             def _():
-                arrived(qbuf, q_recv, s)
-
-        first_row = g * piece_rows
-        half = first_row // block
-        q_block = order[2 * ctx + half]
-        q_pos = q_block * block + (first_row - half * block) + lax.broadcasted_iota(jnp.int32, (piece_rows, total), 0)
-        col = lax.broadcasted_iota(jnp.int32, (piece_rows, total), 1)
-        k_pos = jnp.where(col < block, order[2 * ctx] * block + col, order[2 * ctx + 1] * block + col - block)
-        visible = k_pos <= q_pos
-        for h in range(kv_heads):
-            e = jnp.exp2(scores_of(g, h, ctx)).reshape(per_kv, piece_rows, total)
-            w = jnp.where(visible[None], e, 0.0).reshape(per_kv * piece_rows, total)
-            acc[h] = weighted(w, h, ctx)
-
-        def other(d, carry):
-            c = (ctx + d) % n_ctx
-            low = jnp.where(order[2 * c] <= q_block, 0.0, HIDDEN)
-            high = jnp.where(order[2 * c + 1] <= q_block, 0.0, HIDDEN)
-            for h in range(kv_heads):
-                x = scores_of(g, h, c)
-                w = jnp.concatenate([jnp.exp2(x[:, :block] + low), jnp.exp2(x[:, block:] + high)], axis=1)
-                acc[h] += weighted(w, h, c)
-            return carry
-
-        lax.fori_loop(1, n_ctx, other, 0)
+                arrived(qbuf, q_recv, flip(me, j, n_head))
+
+    def finish(step):
+        first_row = flip(home, step, pieces) * piece_rows
         span = pl.ds(pl.multiple_of(first_row, piece_rows), piece_rows)
         for h in range(kv_heads):
-            a = acc[h]
+            a = acc[step, h]
             o = (a[:, :HEAD_WIDTH] / a[:, HEAD_WIDTH:]).astype(jnp.bfloat16)
             for i in range(per_kv):
                 at = (h * per_kv + i) * HEAD_WIDTH
                 out[span, at : at + HEAD_WIDTH] = o[i * piece_rows : (i + 1) * piece_rows]
-        return carry
-
-    lax.fori_loop(0, pieces, one_group, 0)
+
+    def each(count, body):
+        lax.fori_loop(0, count, lambda i, carry: (body(i), carry)[1], 0)
+
+    near_steps, far_steps = range(near_pieces), range(near_pieces, pieces)
+    for step in near_steps:
+        collect(step)
+    for step in near_steps:
+        relay(flip(home, step, pieces))
+    mine[2].wait()
+    for t in range(chips):
+        others_arrived(t, near_steps)
+
+    def near_near(step):
+        q_arrived(step)
+        unit(step, 0, 0, True)
+        each(chips - 1, lambda t: unit(step, 0, t + 1, False))
+
+    each(near_pieces, near_near)
+    for step in far_steps:
+        collect(step)
+        if step > near_pieces:
+            relay(flip(home, step - 1, pieces))
+    others_arrived(0, far_steps)
+    each(near_pieces, lambda step: unit(step, 1, 0, False))
+    relay(flip(home, pieces - 1, pieces))
+    for t in range(1, chips):
+        others_arrived(t, far_steps)
+
+    def rest(step):
+        each(chips - 1, lambda t: unit(step, 1, t + 1, False))
+        finish(step)
+
+    each(near_pieces, rest)
+
+    def far_all(i):
+        step = near_pieces + i
+        q_arrived(step)
+        unit(step, 1, 0, True)
+        each(2 * chips - 1, lambda u: unit(step, u // chips, u % chips + u // chips, False))
+        finish(step)
+
+    each(near_pieces, far_all)
     for copy in sends:
         copy.wait_send()
     for copy in passed:
@@ -223,7 +262,7 @@
         scratch_shapes=[
             pltpu.VMEM((total, q_cols), jnp.bfloat16),
             pltpu.VMEM((n_ctx, 2, total, kv_cols), jnp.bfloat16),
-            pltpu.VMEM((kv_heads, per_kv * pair * rows, 2 * HEAD_WIDTH), jnp.float32),
+            pltpu.VMEM((pieces, kv_heads, per_kv * pair * rows, 2 * HEAD_WIDTH), jnp.float32),
             dma((n_head,)), dma((n_head,)), dma((n_head,)),
             dma((n_head,)), dma((n_head,)), dma((n_head,)),
             dma((3,)),

time: 57.5 us -> 52.2 us (0.908)
  the two profiles are of different devices: /device:TPU:9 before, /device:TPU:1 now
where the time goes in v2:
time: 52.2 us; the launch traced here: 52 us
  Pallas kernels  49.9 us (96%)
  local copies, waits for them, and re-layouts  2.06 us (4%)
    pallas_call x1, Pallas kernels, shards(): pl.pallas_call(functools.partial(kernel, n_head, n_ctx, pair), out_shape=...  49.9 us
    unnamed x1, local copies, waits for them, and re-layouts  2.06 us

profile of v2, /device:TPU:1, one launch (start us, length us, event | category | flops | bytes accessed | tf_op | source)
XLA Modules:
  0.0 52.0 jit_solution(18380598200049449466)
XLA Ops:
  0.0 49.9 %shard_map.46 = bf16[768,512]{1,0:T(8,128)(2,1)} custom-call(s32[8]{0:T(128)} %order.1, bf16[96,4096]{1,0:T(8,128)(2,1)} %query.1, bf16[96,2048]{1,0:T(8,128)(2,1)} %key.1, bf16[96,2048]{1,0:T(8,128)(2,1)} %value.1), custom_call_target="tpu_custom_call" | custom-call | tf_op jit(solution)/shard_map/pallas_call | solution.py:257
  49.9 2.1 %copy.6 = bf16[768,512]{1,0:T(8,128)(2,1)} copy(bf16[768,512]{1,0:T(8,128)(2,1)} %shard_map.46) | data formatting | bytes 1572864
